TPU v7x, 32 devices: a whole 2x2x4 slice. The times are simulated.
32 devices in a mesh: replica: 16 (over z, y, x), model: 2 (over core).
Axes of the slice: x: 2, y: 2, z: 4, core: 2. Of those that a mesh axis runs over, the one named last changes fastest.
Arguments:
- slope_up: float32 [16, 768, 3072], P('replica', None, 'model'), may hold values from -4 to 4
- slope_down: float32 [16, 3072, 768], P('replica', 'model'), may hold values from -4 to 4
- slope_query: float32 [16, 768, 768], P('replica', None, 'model'), may hold values from -4 to 4
- slope_key: float32 [16, 768, 768], P('replica', None, 'model'), may hold values from -4 to 4
- slope_value: float32 [16, 768, 768], P('replica', None, 'model'), may hold values from -4 to 4
- slope_mixed: float32 [16, 768, 768], P('replica', 'model'), may hold values from -4 to 4
- slope_norm: float32 [16, 768], P('replica'), may hold values from -8 to 8
- slope_bias: float32 [16, 768], P('replica'), may hold values from -8 to 8
- param_up: float32 [768, 3072], P('replica', 'model'), may hold values from -0.3125 to 0.3125
- param_down: float32 [3072, 768], P('model', 'replica'), may hold values from -0.15625 to 0.15625
- param_query: float32 [768, 768], P('replica', 'model'), may hold values from -0.3125 to 0.3125
- param_key: float32 [768, 768], P('replica', 'model'), may hold values from -0.3125 to 0.3125
- param_value: float32 [768, 768], P('replica', 'model'), may hold values from -0.3125 to 0.3125
- param_mixed: float32 [768, 768], P('model', 'replica'), may hold values from -0.3125 to 0.3125
- param_norm: float32 [768], P('replica'), may hold values from 0.25 to 1.75
- param_bias: float32 [768], P('replica'), may hold values from -3 to 3
- state_up: float32 [768, 3072], P('replica', 'model'), may hold values from 0.00026041668 to 0.0026041667
- state_down: float32 [3072, 768], P('model', 'replica'), may hold values from 6.510417e-05 to 0.0006510417
- state_query: float32 [768, 768], P('replica', 'model'), may hold values from 0.00026041668 to 0.0026041667
- state_key: float32 [768, 768], P('replica', 'model'), may hold values from 0.00026041668 to 0.0026041667
- state_value: float32 [768, 768], P('replica', 'model'), may hold values from 0.00026041668 to 0.0026041667
- state_mixed: float32 [768, 768], P('model', 'replica'), may hold values from 0.00026041668 to 0.0026041667
- state_norm: float32 [768], P('replica'), may hold values from 0.05 to 0.8
- state_bias: float32 [768], P('replica'), may hold values from 0.05 to 0.8
Outputs:
- half_up: bfloat16 [768, 3072], P(None, 'model')
- half_down: bfloat16 [3072, 768], P('model')
- half_query: bfloat16 [768, 768], P(None, 'model')
- half_key: bfloat16 [768, 768], P(None, 'model')
- half_value: bfloat16 [768, 768], P(None, 'model')
- half_mixed: bfloat16 [768, 768], P('model')
- half_norm: bfloat16 [768], replicated
- half_bias: bfloat16 [768], replicated
- next_up: float32 [768, 3072], P('replica', 'model')
- next_down: float32 [3072, 768], P('model', 'replica')
- next_query: float32 [768, 768], P('replica', 'model')
- next_key: float32 [768, 768], P('replica', 'model')
- next_value: float32 [768, 768], P('replica', 'model')
- next_mixed: float32 [768, 768], P('model', 'replica')
- next_norm: float32 [768], P('replica')
- next_bias: float32 [768], P('replica')
- state_new_up: float32 [768, 3072], P('replica', 'model')
- state_new_down: float32 [3072, 768], P('model', 'replica')
- state_new_query: float32 [768, 768], P('replica', 'model')
- state_new_key: float32 [768, 768], P('replica', 'model')
- state_new_value: float32 [768, 768], P('replica', 'model')
- state_new_mixed: float32 [768, 768], P('model', 'replica')
- state_new_norm: float32 [768], P('replica')
- state_new_bias: float32 [768], P('replica')
All inputs are finite; a program needn't handle non-finite values.
Results may differ from a plain program's by a relative error of at most 0.001.
Values may be sent and summed in bfloat16 or wider, within the bound.
A program may use at most 64 MiB of HBM per device.

v0:
```python
import jax
import jax.numpy as jnp
from jax import lax
from jax.sharding import PartitionSpec as P

learn_rate = 0.025
hold_rate = 0.7


def on_device(
    slope_up,
    slope_down,
    slope_query,
    slope_key,
    slope_value,
    slope_mixed,
    slope_norm,
    slope_bias,
    param_up,
    param_down,
    param_query,
    param_key,
    param_value,
    param_mixed,
    param_norm,
    param_bias,
    state_up,
    state_down,
    state_query,
    state_key,
    state_value,
    state_mixed,
    state_norm,
    state_bias,
):
    mean_up, mean_down, mean_query, mean_key, mean_value, mean_mixed, mean_norm, mean_bias = (
        lax.psum_scatter(
            slope_up[0].astype(jnp.float32), "replica", scatter_dimension=0, tiled=True
        ),
        lax.psum_scatter(
            slope_down[0].astype(jnp.float32), "replica", scatter_dimension=1, tiled=True
        ),
        lax.psum_scatter(
            slope_query[0].astype(jnp.float32), "replica", scatter_dimension=0, tiled=True
        ),
        lax.psum_scatter(
            slope_key[0].astype(jnp.float32), "replica", scatter_dimension=0, tiled=True
        ),
        lax.psum_scatter(
            slope_value[0].astype(jnp.float32), "replica", scatter_dimension=0, tiled=True
        ),
        lax.psum_scatter(
            slope_mixed[0].astype(jnp.float32), "replica", scatter_dimension=1, tiled=True
        ),
        lax.psum_scatter(
            slope_norm[0].astype(jnp.float32), "replica", scatter_dimension=0, tiled=True
        ),
        lax.psum_scatter(
            slope_bias[0].astype(jnp.float32), "replica", scatter_dimension=0, tiled=True
        ),
    )
    mean_rate = lax.axis_size("replica") ** (-0.5)
    mean_up = mean_up * mean_rate
    mean_down = mean_down * mean_rate
    mean_query = mean_query * mean_rate
    mean_key = mean_key * mean_rate
    mean_value = mean_value * mean_rate
    mean_mixed = mean_mixed * mean_rate
    mean_norm = mean_norm * mean_rate
    mean_bias = mean_bias * mean_rate
    (
        own_up,
        own_down,
        own_query,
        own_key,
        own_value,
        own_mixed,
        slope_up_norm,
        slope_down_norm,
        slope_query_norm,
        slope_key_norm,
        slope_value_norm,
        slope_mixed_norm,
    ) = lax.psum(
        (
            jnp.sum(param_up * param_up, axis=1, keepdims=True),
            jnp.sum(param_down * param_down, axis=0, keepdims=True),
            jnp.sum(param_query * param_query, axis=1, keepdims=True),
            jnp.sum(param_key * param_key, axis=1, keepdims=True),
            jnp.sum(param_value * param_value, axis=1, keepdims=True),
            jnp.sum(param_mixed * param_mixed, axis=0, keepdims=True),
            jnp.sum(mean_up * mean_up, axis=1, keepdims=True),
            jnp.sum(mean_down * mean_down, axis=0, keepdims=True),
            jnp.sum(mean_query * mean_query, axis=1, keepdims=True),
            jnp.sum(mean_key * mean_key, axis=1, keepdims=True),
            jnp.sum(mean_value * mean_value, axis=1, keepdims=True),
            jnp.sum(mean_mixed * mean_mixed, axis=0, keepdims=True),
        ),
        "model",
    )
    mean_up = mean_up * (jnp.sqrt(own_up) * lax.rsqrt(slope_up_norm + 1e-06))
    mean_down = mean_down * (jnp.sqrt(own_down) * lax.rsqrt(slope_down_norm + 1e-06))
    mean_query = mean_query * (jnp.sqrt(own_query) * lax.rsqrt(slope_query_norm + 1e-06))
    mean_key = mean_key * (jnp.sqrt(own_key) * lax.rsqrt(slope_key_norm + 1e-06))
    mean_value = mean_value * (jnp.sqrt(own_value) * lax.rsqrt(slope_value_norm + 1e-06))
    mean_mixed = mean_mixed * (jnp.sqrt(own_mixed) * lax.rsqrt(slope_mixed_norm + 1e-06))
    state_new_up = hold_rate * state_up + (1.0 - hold_rate) * mean_up * mean_up
    next_up = param_up - learn_rate * mean_up * lax.rsqrt(state_new_up + 1e-06)
    state_new_down = hold_rate * state_down + (1.0 - hold_rate) * mean_down * mean_down
    next_down = param_down - learn_rate * mean_down * lax.rsqrt(state_new_down + 1e-06)
    state_new_query = hold_rate * state_query + (1.0 - hold_rate) * mean_query * mean_query
    next_query = param_query - learn_rate * mean_query * lax.rsqrt(state_new_query + 1e-06)
    state_new_key = hold_rate * state_key + (1.0 - hold_rate) * mean_key * mean_key
    next_key = param_key - learn_rate * mean_key * lax.rsqrt(state_new_key + 1e-06)
    state_new_value = hold_rate * state_value + (1.0 - hold_rate) * mean_value * mean_value
    next_value = param_value - learn_rate * mean_value * lax.rsqrt(state_new_value + 1e-06)
    state_new_mixed = hold_rate * state_mixed + (1.0 - hold_rate) * mean_mixed * mean_mixed
    next_mixed = param_mixed - learn_rate * mean_mixed * lax.rsqrt(state_new_mixed + 1e-06)
    state_new_norm = hold_rate * state_norm + (1.0 - hold_rate) * mean_norm * mean_norm
    next_norm = param_norm - learn_rate * mean_norm * lax.rsqrt(state_new_norm + 1e-06)
    state_new_bias = hold_rate * state_bias + (1.0 - hold_rate) * mean_bias * mean_bias
    next_bias = param_bias - learn_rate * mean_bias * lax.rsqrt(state_new_bias + 1e-06)
    half_up, half_down, half_query, half_key, half_value, half_mixed, half_norm, half_bias = (
        lax.all_gather(next_up.astype(jnp.bfloat16), "replica", axis=0, tiled=True),
        lax.all_gather(next_down.astype(jnp.bfloat16), "replica", axis=1, tiled=True),
        lax.all_gather(next_query.astype(jnp.bfloat16), "replica", axis=0, tiled=True),
        lax.all_gather(next_key.astype(jnp.bfloat16), "replica", axis=0, tiled=True),
        lax.all_gather(next_value.astype(jnp.bfloat16), "replica", axis=0, tiled=True),
        lax.all_gather(next_mixed.astype(jnp.bfloat16), "replica", axis=1, tiled=True),
        lax.all_gather(next_norm.astype(jnp.bfloat16), "replica", axis=0, tiled=True),
        lax.all_gather(next_bias.astype(jnp.bfloat16), "replica", axis=0, tiled=True),
    )
    return (
        half_up,
        half_down,
        half_query,
        half_key,
        half_value,
        half_mixed,
        half_norm,
        half_bias,
        next_up,
        next_down,
        next_query,
        next_key,
        next_value,
        next_mixed,
        next_norm,
        next_bias,
        state_new_up,
        state_new_down,
        state_new_query,
        state_new_key,
        state_new_value,
        state_new_mixed,
        state_new_norm,
        state_new_bias,
    )


def solution(mesh):
    return jax.shard_map(
        on_device,
        mesh=mesh,
        in_specs=(
            P("replica", None, "model"),
            P("replica", "model", None),
            P("replica", None, "model"),
            P("replica", None, "model"),
            P("replica", None, "model"),
            P("replica", "model", None),
            P("replica", None),
            P("replica", None),
            P("replica", "model"),
            P("model", "replica"),
            P("replica", "model"),
            P("replica", "model"),
            P("replica", "model"),
            P("model", "replica"),
            P("replica"),
            P("replica"),
            P("replica", "model"),
            P("model", "replica"),
            P("replica", "model"),
            P("replica", "model"),
            P("replica", "model"),
            P("model", "replica"),
            P("replica"),
            P("replica"),
        ),
        out_specs=(
            P(None, "model"),
            P("model", None),
            P(None, "model"),
            P(None, "model"),
            P(None, "model"),
            P("model", None),
            P(),
            P(),
            P("replica", "model"),
            P("model", "replica"),
            P("replica", "model"),
            P("replica", "model"),
            P("replica", "model"),
            P("model", "replica"),
            P("replica"),
            P("replica"),
            P("replica", "model"),
            P("model", "replica"),
            P("replica", "model"),
            P("replica", "model"),
            P("replica", "model"),
            P("model", "replica"),
            P("replica"),
            P("replica"),
        ),
        check_vma=False,
    )
```

profile of v0, /device:TPU:0, one launch (start us, length us, event | category | flops | bytes accessed | tf_op | source)
XLA Modules:
  0.0 1086.5 jit_solution(11323618748119882401)
XLA Ops:
  9.5 1.4 copy.53
  11.5 6.0 copy.52
  19.3 121.2 %reduce-scatter.11.cloned.1.call-done = f32[48,384]{1,0:T(8,128)} async-done(((f32[768,384]{1,0:T(8,128)}), f32[48,384]{1,0:T(8,128)}) %reduce-scatter.11.cloned.1.call-update) | async-done | bytes 73744 | tf_op jit(solution)/shard_map/reduce_scatter | solution.py:43
  140.5 1.1 multiply_reduce_fusion.10
  141.6 127.8 %reduce-scatter.13.cloned.1.call-done = f32[48,384]{1,0:T(8,128)} async-done(((f32[768,384]{1,0:T(8,128)}), f32[48,384]{1,0:T(8,128)}) %reduce-scatter.13.cloned.1.call-update) | async-done | bytes 73744 | tf_op jit(solution)/shard_map/reduce_scatter | solution.py:46
  269.4 1.0 multiply_reduce_fusion.8
  270.3 127.9 %reduce-scatter.15.cloned.1.call-done = f32[48,384]{1,0:T(8,128)} async-done(((f32[768,384]{1,0:T(8,128)}), f32[48,384]{1,0:T(8,128)}) %reduce-scatter.15.cloned.1.call-update) | async-done | bytes 73744 | tf_op jit(solution)/shard_map/reduce_scatter | solution.py:49
  399.3 128.1 %reduce-scatter.17.cloned.1.call-done = f32[384,48]{0,1:T(8,128)} async-done(((f32[384,768]{0,1:T(8,128)}), f32[384,48]{0,1:T(8,128)}) %reduce-scatter.17.cloned.1.call-update) | async-done | bytes 73744 | tf_op jit(solution)/shard_map/reduce_scatter | solution.py:52
  528.4 142.2 %reduce-scatter.7.cloned.1.call-done = f32[48,1536]{1,0:T(8,128)} async-done(((f32[768,1536]{1,0:T(8,128)}), f32[48,1536]{1,0:T(8,128)}) %reduce-scatter.7.cloned.1.call-update) | async-done | bytes 294928 | tf_op jit(solution)/shard_map/reduce_scatter | solution.py:37
  670.6 1.1 multiply_reduce_fusion.2
  671.7 142.2 %reduce-scatter.9.cloned.1.call-done = f32[1536,48]{0,1:T(8,128)} async-done(((f32[1536,768]{0,1:T(8,128)}), f32[1536,48]{0,1:T(8,128)}) %reduce-scatter.9.cloned.1.call-update) | async-done | bytes 294928 | tf_op jit(solution)/shard_map/reduce_scatter | solution.py:40
  813.9 1.1 multiply_reduce_fusion
  815.0 2.5 all-reduce.5
  817.5 2.0 fusion.18
  819.7 2.0 fusion.16
  823.7 40.2 %all-reduce.4 = (f32[768]{0:T(1024)S(1)}, f32[768]{0:T(1024)S(1)}) all-reduce(f32[768]{0:T(1024)S(1)} %reduce, f32[768]{0:T(1024)S(1)} %reduce.1), channel_id=8, replica_groups=mesh['replica'=16,'model'=2] {'replica'}, use_global_device_ids=true, to_apply=%region_30.0.clone | all-reduce | flops 1536 | bytes 12288
  864.9 37.5 %all-reduce.6 = (bf16[768]{0:T(1024)(128)(2,1)}, bf16[768]{0:T(1024)(128)(2,1)}) all-reduce(bf16[768]{0:T(1024)(128)(2,1)S(1)} %dynamic-update-slice, bf16[768]{0:T(1024)(128)(2,1)S(1)} %dynamic-update-slice.1), channel_id=1, replica_groups=mesh['replica'=16,'model'=2] {'replica'}, use_global_device_ids=true, to_apply=%add | all-reduce | flops 1536 | bytes 6144
  903.1 43.5 %all_gather.26 = bf16[768,384]{1,0:T(8,128)(2,1)S(1)} all-gather(bf16[48,384]{1,0:T(8,128)(2,1)S(1)} %get-tuple-element.103), channel_id=1, replica_groups=mesh['replica'=16,'model'=2] {'replica'}, dimensions={0}, use_global_device_ids=true | all-gather | bytes 626688 | tf_op jit(solution)/shard_map/all_gather | solution.py:126
  947.4 39.9 %all_gather.27 = bf16[768,384]{1,0:T(8,128)(2,1)S(1)} all-gather(bf16[48,384]{1,0:T(8,128)(2,1)S(1)} %get-tuple-element.100), channel_id=1, replica_groups=mesh['replica'=16,'model'=2] {'replica'}, dimensions={0}, use_global_device_ids=true | all-gather | bytes 626688 | tf_op jit(solution)/shard_map/all_gather | solution.py:127
  988.0 42.4 %all_gather.28 = bf16[768,384]{1,0:T(8,128)(2,1)} all-gather(bf16[48,384]{1,0:T(8,128)(2,1)S(1)} %get-tuple-element.97), channel_id=1, replica_groups=mesh['replica'=16,'model'=2] {'replica'}, dimensions={0}, use_global_device_ids=true | all-gather | bytes 626688 | tf_op jit(solution)/shard_map/all_gather | solution.py:128
  1031.2 39.1 %all_gather.29 = bf16[384,768]{0,1:T(8,128)(2,1)S(1)} all-gather(bf16[384,48]{0,1:T(8,128)(2,1)S(1)} %get-tuple-element.94), channel_id=1, replica_groups=mesh['replica'=16,'model'=2] {'replica'}, dimensions={1}, use_global_device_ids=true | all-gather | bytes 626688 | tf_op jit(solution)/shard_map/all_gather | solution.py:129
  1070.3 1.1 copy.55
  1071.4 4.4 copy.54
  1075.8 1.4 copy.62
  (96 shorter events, 13.6 us)
Async XLA Ops:
  7.2 133.3 %reduce-scatter.11.cloned.1.call-start = ((), (), s32[]{:S(2)}) async-start(), calls=%async_computation.10 | async-start | bytes 1253376 | tf_op jit(solution)/shard_map/reduce_scatter | solution.py:43
  7.9 261.4 %reduce-scatter.13.cloned.1.call-start = ((), (), s32[]{:S(2)}) async-start(), calls=%async_computation.11 | async-start | bytes 1253376 | tf_op jit(solution)/shard_map/reduce_scatter | solution.py:46
  8.7 389.6 %reduce-scatter.15.cloned.1.call-start = ((), (), s32[]{:S(2)}) async-start(), calls=%async_computation.12 | async-start | bytes 1253376 | tf_op jit(solution)/shard_map/reduce_scatter | solution.py:49
  9.4 518.0 %reduce-scatter.17.cloned.1.call-start = ((), (), s32[]{:S(2)}) async-start(), calls=%async_computation.13 | async-start | bytes 1253376 | tf_op jit(solution)/shard_map/reduce_scatter | solution.py:52
  10.9 659.7 %reduce-scatter.7.cloned.1.call-start = ((), (), s32[]{:S(2)}) async-start(), calls=%async_computation.6 | async-start | bytes 5013504 | tf_op jit(solution)/shard_map/reduce_scatter | solution.py:37
  11.5 802.4 %reduce-scatter.9.cloned.1.call-start = ((), (), s32[]{:S(2)}) async-start(), calls=%async_computation.8 | async-start | bytes 5013504 | tf_op jit(solution)/shard_map/reduce_scatter | solution.py:40
  17.6 799.9 %copy-start.13 = (f32[48,1536]{1,0:T(8,128)S(1)}, f32[48,1536]{1,0:T(8,128)}, u32[]{:S(2)}) copy-start(f32[48,1536]{1,0:T(8,128)} %param.40) | copy-start | bytes 884740
  17.6 802.0 %copy-start.14 = (f32[1536,48]{0,1:T(8,128)S(1)}, f32[1536,48]{0,1:T(8,128)}, u32[]{:S(2)}) copy-start(f32[1536,48]{0,1:T(8,128)} %param.41) | copy-start | bytes 884740
  17.7 1053.7 %all-gather.3.cloned.1.call-start = ((), (), s32[]{:S(2)}) async-start(), calls=%async_computation.7 | async-start | bytes 2506752 | tf_op jit(solution)/shard_map/all_gather | solution.py:124
  19.1 802.7 %copy-start.19 = (f32[1,768]{1,0:T(1,128)S(1)}, f32[1,768]{1,0:T(1,128)}, u32[]{:S(2)}) copy-start(f32[1,768]{1,0:T(1,128)} %param.30) | copy-start | bytes 9220
  19.1 802.7 %copy-start.20 = (f32[1,768]{1,0:T(1,128)S(1)}, f32[1,768]{1,0:T(1,128)}, u32[]{:S(2)}) copy-start(f32[1,768]{1,0:T(1,128)} %param.31) | copy-start | bytes 9220
  19.1 802.7 %copy-start.21 = (u32[32]{0:T(128)S(1)}, u32[32]{0:T(128)}, u32[]{:S(2)}) copy-start(u32[32]{0:T(128)} %constant.22) | copy-start | bytes 388
  19.1 844.8 %copy-start.22 = (f32[48]{0:T(128)S(1)}, f32[48]{0:T(128)}, u32[]{:S(2)}) copy-start(f32[48]{0:T(128)} %param.39) | copy-start | bytes 580
  19.1 844.8 %copy-start.23 = (f32[48]{0:T(128)S(1)}, f32[48]{0:T(128)}, u32[]{:S(2)}) copy-start(f32[48]{0:T(128)} %param.47) | copy-start | bytes 580
  19.1 844.8 %copy-start.24 = (f32[48]{0:T(128)S(1)}, f32[48]{0:T(128)}, u32[]{:S(2)}) copy-start(f32[48]{0:T(128)} %param.38) | copy-start | bytes 580
  19.1 844.7 %copy-start.25 = (f32[48]{0:T(128)S(1)}, f32[48]{0:T(128)}, u32[]{:S(2)}) copy-start(f32[48]{0:T(128)} %param.46) | copy-start | bytes 580
  19.3 883.1 %copy-start.15 = (f32[48,384]{1,0:T(8,128)S(1)}, f32[48,384]{1,0:T(8,128)}, u32[]{:S(2)}) copy-start(f32[48,384]{1,0:T(8,128)} %param.42) | copy-start | bytes 221188
  140.5 761.8 %copy-start.12 = (f32[48,384]{1,0:T(8,128)S(1)}, f32[48,384]{1,0:T(8,128)}, u32[]{:S(2)}) copy-start(f32[48,384]{1,0:T(8,128)} %reduce-scatter.11.cloned.1.call-done) | copy-start | bytes 221188
  817.5 129.2 %copy-start.16 = (f32[48,384]{1,0:T(8,128)S(1)}, f32[48,384]{1,0:T(8,128)}, u32[]{:S(2)}) copy-start(f32[48,384]{1,0:T(8,128)} %param.43) | copy-start | bytes 221188
  819.5 167.7 %copy-start.10 = (f32[48,384]{1,0:T(8,128)S(1)}, f32[48,384]{1,0:T(8,128)}, u32[]{:S(2)}) copy-start(f32[48,384]{1,0:T(8,128)} %reduce-scatter.15.cloned.1.call-done) | copy-start | bytes 221188
  819.5 167.7 %copy-start.17 = (f32[48,384]{1,0:T(8,128)S(1)}, f32[48,384]{1,0:T(8,128)}, u32[]{:S(2)}) copy-start(f32[48,384]{1,0:T(8,128)} %param.44) | copy-start | bytes 221188
  819.6 251.8 %all-gather.5.cloned.1.call-start = ((), (), s32[]{:S(2)}) async-start(), calls=%async_computation.9 | async-start | bytes 2506752 | tf_op jit(solution)/shard_map/all_gather | solution.py:125
  819.6 210.8 %copy-start.11 = (f32[384,48]{0,1:T(8,128)S(1)}, f32[384,48]{0,1:T(8,128)}, u32[]{:S(2)}) copy-start(f32[384,48]{0,1:T(8,128)} %reduce-scatter.17.cloned.1.call-done) | copy-start | bytes 221188
  819.7 210.8 %copy-start.18 = (f32[384,48]{0,1:T(8,128)S(1)}, f32[384,48]{0,1:T(8,128)}, u32[]{:S(2)}) copy-start(f32[384,48]{0,1:T(8,128)} %param.45) | copy-start | bytes 221188
  (10 other events, 144.5 us)
Sparse Core Ops, SparseCore 0:
  12.8 127.7 reduce-scatter.10
  145.3 124.0 reduce-scatter.12
  274.1 124.1 reduce-scatter.14
  403.5 123.9 reduce-scatter.16
  532.5 138.1 reduce-scatter.6
  675.6 138.1 reduce-scatter.8
  819.7 61.9 all-gather.2
  885.0 65.9 all-gather.4
where the time goes:
time: 1090 us
  waiting for transfers between devices  792 us (73%)
  blocking collectives  245 us (22%)
  local copies, waits for them, and re-layouts  18.6 us (2%)
  between operations  15.8 us (1%)
  other arithmetic  14.6 us (1%)
    reduce_scatter x1, waiting for transfers between devices, on_device(): lax.psum_scatter(slope_up[0].astype(jnp.float32), 'replica', scatter_dime...  142 us
    reduce_scatter x1, waiting for transfers between devices, on_device(): lax.psum_scatter(slope_down[0].astype(jnp.float32), 'replica', scatter_di...  142 us
    reduce_scatter x1, waiting for transfers between devices, on_device(): lax.psum_scatter(slope_mixed[0].astype(jnp.float32), 'replica', scatter_d...  128 us
    reduce_scatter x1, waiting for transfers between devices, on_device(): lax.psum_scatter(slope_value[0].astype(jnp.float32), 'replica', scatter_d...  128 us
    reduce_scatter x1, waiting for transfers between devices, on_device(): lax.psum_scatter(slope_key[0].astype(jnp.float32), 'replica', scatter_dim...  128 us
    reduce_scatter x1, waiting for transfers between devices, on_device(): lax.psum_scatter(slope_query[0].astype(jnp.float32), 'replica', scatter_d...  121 us
    unnamed x2, blocking collectives  77.6 us
    all_gather x1, blocking collectives, on_device(): lax.all_gather(next_query.astype(jnp.bfloat16), 'replica', axis=0, tiled=...  43.5 us
  transfers between devices with their start and end apart: 8, of which 6 were waited for; matrix products, arithmetic and copies ran while one was open for 2% of the time, Pallas kernels for 0%

commit v1 on v0

--- a/solution.py
+++ b/solution.py
@@ -1,10 +1,75 @@
 import jax
 import jax.numpy as jnp
 from jax import lax
+from jax.experimental import pallas as pl
 from jax.sharding import PartitionSpec as P
 
 learn_rate = 0.025
 hold_rate = 0.7
+LANES = 128
+TURNED = (1, 5)
+
+
+def lane_ceil(width):
+    return -(-width // LANES) * LANES
+
+
+def split_columns(packed, widths, steps):
+    pieces, start = [], 0
+    for width, step in zip(widths, steps):
+        pieces.append(packed[:, start : start + width])
+        start += step
+    return pieces
+
+
+def pack_kernel(*refs):
+    out_ref = refs[-1]
+    start = 0
+    for at, ref in enumerate(refs[:-1]):
+        block = ref[...].T if at in TURNED else ref[...]
+        width = block.shape[1]
+        out_ref[:, start : start + width] = block
+        step = lane_ceil(width)
+        if step > width:
+            out_ref[:, start + width : start + step] = jnp.zeros(
+                (block.shape[0], step - width), block.dtype
+            )
+        start += step
+
+
+def pack_slopes(*arrays):
+    rows = arrays[0].shape[1]
+    tile = LANES if rows % LANES == 0 else rows
+    specs, total = [], 0
+    for at, array in enumerate(arrays):
+        if at in TURNED:
+            specs.append(pl.BlockSpec((None, array.shape[1], tile), lambda i: (0, 0, i)))
+            total += lane_ceil(array.shape[1])
+        elif array.ndim == 3:
+            specs.append(pl.BlockSpec((None, tile, array.shape[2]), lambda i: (0, i, 0)))
+            total += lane_ceil(array.shape[2])
+        else:
+            specs.append(pl.BlockSpec((tile, array.shape[1]), lambda i: (i, 0)))
+            total += lane_ceil(array.shape[1])
+    return pl.pallas_call(
+        pack_kernel,
+        grid=(rows // tile,),
+        in_specs=specs,
+        out_specs=pl.BlockSpec((tile, total), lambda i: (i, 0)),
+        out_shape=jax.ShapeDtypeStruct((rows, total), jnp.float32),
+        cost_estimate=pl.CostEstimate(
+            flops=0, bytes_accessed=8 * rows * total, transcendentals=0
+        ),
+        name="pack_slopes",
+    )(*arrays)
+
+
+def scatter_sum(packed):
+    return lax.psum_scatter(packed, "replica", scatter_dimension=0, tiled=True)
+
+
+def gather_rows(packed):
+    return lax.all_gather(packed, "replica", axis=0, tiled=True)
 
 
 def on_device(
@@ -33,32 +98,33 @@
     state_norm,
     state_bias,
 ):
+    packed = pack_slopes(
+        slope_up,
+        slope_down,
+        slope_query,
+        slope_key,
+        slope_value,
+        slope_mixed,
+        jnp.pad(jnp.stack([slope_norm[0], slope_bias[0]], axis=1), ((0, 0), (0, LANES - 2))),
+    )
+    packed = scatter_sum(packed)
+    widths = (
+        slope_up.shape[2],
+        slope_down.shape[1],
+        slope_query.shape[2],
+        slope_key.shape[2],
+        slope_value.shape[2],
+        slope_mixed.shape[1],
+        1,
+        1,
+    )
     mean_up, mean_down, mean_query, mean_key, mean_value, mean_mixed, mean_norm, mean_bias = (
-        lax.psum_scatter(
-            slope_up[0].astype(jnp.float32), "replica", scatter_dimension=0, tiled=True
-        ),
-        lax.psum_scatter(
-            slope_down[0].astype(jnp.float32), "replica", scatter_dimension=1, tiled=True
-        ),
-        lax.psum_scatter(
-            slope_query[0].astype(jnp.float32), "replica", scatter_dimension=0, tiled=True
-        ),
-        lax.psum_scatter(
-            slope_key[0].astype(jnp.float32), "replica", scatter_dimension=0, tiled=True
-        ),
-        lax.psum_scatter(
-            slope_value[0].astype(jnp.float32), "replica", scatter_dimension=0, tiled=True
-        ),
-        lax.psum_scatter(
-            slope_mixed[0].astype(jnp.float32), "replica", scatter_dimension=1, tiled=True
-        ),
-        lax.psum_scatter(
-            slope_norm[0].astype(jnp.float32), "replica", scatter_dimension=0, tiled=True
-        ),
-        lax.psum_scatter(
-            slope_bias[0].astype(jnp.float32), "replica", scatter_dimension=0, tiled=True
-        ),
-    )
+        split_columns(packed, widths, [lane_ceil(width) for width in widths[:6]] + [1, 1])
+    )
+    mean_down = mean_down.T
+    mean_mixed = mean_mixed.T
+    mean_norm = mean_norm[:, 0]
+    mean_bias = mean_bias[:, 0]
     mean_rate = lax.axis_size("replica") ** (-0.5)
     mean_up = mean_up * mean_rate
     mean_down = mean_down * mean_rate
@@ -120,16 +186,27 @@
     next_norm = param_norm - learn_rate * mean_norm * lax.rsqrt(state_new_norm + 1e-06)
     state_new_bias = hold_rate * state_bias + (1.0 - hold_rate) * mean_bias * mean_bias
     next_bias = param_bias - learn_rate * mean_bias * lax.rsqrt(state_new_bias + 1e-06)
+    packed = jnp.concatenate(
+        [
+            next_up,
+            next_down.T,
+            next_query,
+            next_key,
+            next_value,
+            next_mixed.T,
+            next_norm[:, None],
+            next_bias[:, None],
+        ],
+        axis=1,
+    ).astype(jnp.bfloat16)
+    packed = gather_rows(packed)
     half_up, half_down, half_query, half_key, half_value, half_mixed, half_norm, half_bias = (
-        lax.all_gather(next_up.astype(jnp.bfloat16), "replica", axis=0, tiled=True),
-        lax.all_gather(next_down.astype(jnp.bfloat16), "replica", axis=1, tiled=True),
-        lax.all_gather(next_query.astype(jnp.bfloat16), "replica", axis=0, tiled=True),
-        lax.all_gather(next_key.astype(jnp.bfloat16), "replica", axis=0, tiled=True),
-        lax.all_gather(next_value.astype(jnp.bfloat16), "replica", axis=0, tiled=True),
-        lax.all_gather(next_mixed.astype(jnp.bfloat16), "replica", axis=1, tiled=True),
-        lax.all_gather(next_norm.astype(jnp.bfloat16), "replica", axis=0, tiled=True),
-        lax.all_gather(next_bias.astype(jnp.bfloat16), "replica", axis=0, tiled=True),
-    )
+        split_columns(packed, widths, widths)
+    )
+    half_down = half_down.T
+    half_mixed = half_mixed.T
+    half_norm = half_norm[:, 0]
+    half_bias = half_bias[:, 0]
     return (
         half_up,
         half_down,

time: 1090 us -> 385 us (0.35)
  waiting for transfers between devices: 792 us -> 327 us
  blocking collectives: 245 us -> 4.23 us
  Pallas kernels: 0 us -> 11.8 us
    reduce_scatter x6 -> x1, waiting for transfers between devices: 789 us -> 225 us  [scatter_sum(): return lax.psum_scatter(packed, 'replica', scatter_dimension=0, tiled=True)]
    all_gather x4 -> x0, blocking collectives: 165 us -> none  [the longest x1 43.5 us: on_device(): lax.all_gather(next_query.astype(jnp.bfloat16), 'replica', axis=0, tiled=...]
    all_gather x2 -> x1, waiting for transfers between devices: 0.01 us -> 102 us  [gather_rows(): return lax.all_gather(packed, 'replica', axis=0, tiled=True)]
    unnamed x2 -> x0, blocking collectives: 77.6 us -> none
    unnamed x65 -> x36, local copies, waits for them, and re-layouts: 18.6 us -> 4.26 us
    pallas_call x0 -> x1, Pallas kernels: none -> 11.8 us  [pack_slopes(): pl.pallas_call(pack_kernel, grid=(rows // tile,), in_specs=specs, out_spe...]
  transfers between devices with their start and end apart: 8 -> 2, of which waited for: 6 -> 2; matrix products, arithmetic and copies ran while one was open for 2% -> 0% of each run, Pallas kernels for 0% -> 0%
where the time goes in v1:
time: 385 us; the launch traced here: 384 us
  waiting for transfers between devices  327 us (85%)
  local copies, waits for them, and re-layouts  15.9 us (4%)
  between operations  14.3 us (4%)
  Pallas kernels  11.8 us (3%)
  other arithmetic  11.2 us (3%)
  blocking collectives  4.23 us (1%)
    reduce_scatter x1, waiting for transfers between devices, scatter_sum(): return lax.psum_scatter(packed, 'replica', scatter_dimension=0, tiled=True)  225 us
    all_gather x1, waiting for transfers between devices, gather_rows(): return lax.all_gather(packed, 'replica', axis=0, tiled=True)  102 us
    pallas_call x1, Pallas kernels, pack_slopes(): pl.pallas_call(pack_kernel, grid=(rows // tile,), in_specs=specs, out_spe...  11.8 us
  transfers between devices with their start and end apart: 2, of which 2 were waited for; matrix products, arithmetic and copies ran while one was open for 0% of the time, Pallas kernels for 0%

profile of v1, /device:TPU:0, one launch (start us, length us, event | category | flops | bytes accessed | tf_op | source)
XLA Modules:
  0.0 384.4 jit_solution(18088223597278069342)
XLA Ops:
  7.2 0.7 pad_maximum_fusion
  8.0 0.2 copy.74
  8.1 0.8 pad.4.refs_6_
  8.9 11.8 %pack_slopes.1 = f32[768,4736]{1,0:T(8,128)} custom-call(f32[1,768,1536]{2,1,0:T(8,128)} %refs_0_.1, f32[1,1536,768]{2,1,0:T(8,128)} %refs_1_.1, f32[1,768,384]{2,1,0:T(8,128)} %refs_2_.1, f32[1,768,384]{2,1,0:T(8,128)} %refs_3_.1, f32[1,768,384]{2,1,0:T(8,128)} %refs_4_.1, f32[1,384,768]{2,1,0:T(8,128)} %refs_5_.1, f32[768,128]{1,0:T(8,128)} %pad.4.refs_6_), custom_call_target="tpu_custom_call" | custom-call | bytes 29097984 | tf_op jit(solution)/shard_map/pack_slopes/pallas_call | solution.py:54
  20.9 0.7 copy-done.5
  22.3 0.1 multiply_reduce_fusion.3
  22.6 0.1 multiply_reduce_fusion.1
  22.7 224.8 %reduce-scatter.2.cloned.1.call-done = f32[48,4736]{1,0:T(8,128)} async-done(((f32[768,4736]{1,0:T(8,128)}), f32[48,4736]{1,0:T(8,128)}) %reduce-scatter.2.cloned.1.call-update) | async-done | bytes 909328 | tf_op jit(solution)/shard_map/reduce_scatter | solution.py:68
  247.5 1.1 multiply_reduce_fusion.12
  248.7 0.5 convert_bitcast_fusion.2
  249.4 1.2 multiply_reduce_fusion.4
  250.7 1.3 multiply_reduce_fusion
  252.2 4.2 %all-reduce.1 = (f32[48,1]{1,0:T(8,128)S(1)}, f32[48,1]{1,0:T(8,128)S(1)}, f32[1,48]{1,0:T(1,128)S(1)}, f32[1,48]{1,0:T(1,128)S(1)}, f32[48,1]{1,0:T(8,128)S(1)}...) all-reduce(f32[48,1]{1,0:T(8,128)S(1)} %copy.76, ...), channel_id=1, replica_groups=mesh['replica'=16,'model'=2] {'model'}, use_global_device_ids=true, to_apply=%region_4.5 | all-reduce | flops 576 | bytes 4608 | tf_op jit(solution)/shard_map/psum | solution.py:150
  256.7 1.6 convert_bitcast_fusion.1
  258.4 1.9 convert_bitcast_fusion
  260.3 1.0 fusion.20
  261.3 0.9 fusion.12
  262.2 0.9 concatenate.4
  263.1 102.1 %all-gather.2.cloned.1.call-done = bf16[768,4610]{1,0:T(8,128)(2,1)} async-done(((bf16[48,4610]{1,0:T(8,128)(2,1)}), bf16[768,4610]{1,0:T(8,128)(2,1)}) %all-gather.2.cloned.1.call-update) | async-done | bytes 7080976 | tf_op jit(solution)/shard_map/all_gather | solution.py:72
  365.2 4.1 %slice_bitcast_fusion = (bf16[1536,768]{0,1:T(8,128)(2,1)S(1)}, bf16[768,1536]{1,0:T(8,128)(2,1)}) fusion(bf16[768,4610]{1,0:T(8,128)(2,1)} %all-gather.2.cloned.1.call-done), kind=kLoop, calls=%fused_computation | loop fusion | bytes 9437184 | tf_op jit(solution)/shard_map/transpose | solution.py:206
  369.3 2.4 copy.85
  371.7 2.9 slice_bitcast_fusion.1
  374.6 1.1 copy.86
  375.6 1.9 slice_reduce_fusion
  (54 shorter events, 1.9 us)
Async XLA Ops:
  7.2 240.3 %reduce-scatter.2.cloned.1.call-start = ((), (), s32[]{:S(2)}) async-start(), calls=%async_computation.1 | async-start | bytes 15458304 | tf_op jit(solution)/shard_map/reduce_scatter | solution.py:68
  20.7 0.9 copy-start.5
  20.7 1.1 copy-start.4
  20.7 1.3 copy-start.3
  20.8 1.5 copy-start.2
  20.8 1.7 copy-start.6
  20.8 1.8 copy-start.1
  20.8 227.8 %copy-start.13 = (f32[48]{0:T(128)S(1)}, f32[48]{0:T(128)}, u32[]{:S(2)}) copy-start(f32[48]{0:T(128)} %param.39) | copy-start | bytes 580
  20.8 227.8 %copy-start.14 = (f32[48]{0:T(128)S(1)}, f32[48]{0:T(128)}, u32[]{:S(2)}) copy-start(f32[48]{0:T(128)} %param.47) | copy-start | bytes 580
  20.8 227.8 %copy-start.15 = (f32[48]{0:T(128)S(1)}, f32[48]{0:T(128)}, u32[]{:S(2)}) copy-start(f32[48]{0:T(128)} %param.38) | copy-start | bytes 580
  20.8 227.8 %copy-start.16 = (f32[48]{0:T(128)S(1)}, f32[48]{0:T(128)}, u32[]{:S(2)}) copy-start(f32[48]{0:T(128)} %param.46) | copy-start | bytes 580
  20.9 235.9 %copy-start.12 = (f32[384,48]{0,1:T(8,128)S(1)}, f32[384,48]{0,1:T(8,128)}, u32[]{:S(2)}) copy-start(f32[384,48]{0,1:T(8,128)} %param.45) | copy-start | bytes 221188
  20.9 237.5 %copy-start.7 = (f32[1536,48]{0,1:T(8,128)S(1)}, f32[1536,48]{0,1:T(8,128)}, u32[]{:S(2)}) copy-start(f32[1536,48]{0,1:T(8,128)} %param.41) | copy-start | bytes 884740
  20.9 239.4 %copy-start.8 = (f32[48,1536]{1,0:T(8,128)S(1)}, f32[48,1536]{1,0:T(8,128)}, u32[]{:S(2)}) copy-start(f32[48,1536]{1,0:T(8,128)} %param.40) | copy-start | bytes 884740
  20.9 344.3 %all-gather.2.cloned.1.call-start = ((), (), s32[]{:S(2)}) async-start(), calls=%async_computation.2 | async-start | bytes 7729152 | tf_op jit(solution)/shard_map/all_gather | solution.py:72
  247.5 12.8 %copy-start = (f32[48,4736]{1,0:T(8,128)S(1)}, f32[48,4736]{1,0:T(8,128)}, u32[]{:S(2)}) copy-start(f32[48,4736]{1,0:T(8,128)} %reduce-scatter.2.cloned.1.call-done) | copy-start | bytes 2727940
  250.7 10.7 %copy-start.9 = (f32[48,384]{1,0:T(8,128)S(1)}, f32[48,384]{1,0:T(8,128)}, u32[]{:S(2)}) copy-start(f32[48,384]{1,0:T(8,128)} %param.44) | copy-start | bytes 221188
  250.7 10.7 %copy-start.10 = (f32[48,384]{1,0:T(8,128)S(1)}, f32[48,384]{1,0:T(8,128)}, u32[]{:S(2)}) copy-start(f32[48,384]{1,0:T(8,128)} %param.43) | copy-start | bytes 221188
  250.7 10.6 %copy-start.11 = (f32[48,384]{1,0:T(8,128)S(1)}, f32[48,384]{1,0:T(8,128)}, u32[]{:S(2)}) copy-start(f32[48,384]{1,0:T(8,128)} %param.42) | copy-start | bytes 221188
Sparse Core Ops, SparseCore 0:
  21.0 226.4 reduce-scatter.1
  263.2 101.8 all-gather.1
